TPU v7x, 32 devices: a whole 2x2x4 slice. The times are simulated.
32 devices in a mesh: band: 8 (over z, x), gvec: 4 (over y, core).
Axes of the slice: x: 2, y: 2, z: 4, core: 2. Of those that a mesh axis runs over, the one named last changes fastest.
Arguments:
- wave_coeffs: bfloat16 [2, 256, 75264], P(None, 'band', 'gvec'), may hold values from -6 to 6
- projectors: bfloat16 [2, 64, 75264], P(None, 'band', 'gvec'), may hold values from -0.0234375 to 0.0234375
- miller_index: int32 [3, 75264], P(None, 'gvec'), may hold values from -24 to 24
- lattice: float32 [3, 3], replicated, may hold values from -0.25 to 1.25
- occupation: float32 [256], P('band'), may hold values from 0 to 2
- species: int32 [8], replicated, may hold values from 0 to 3
- proj_count: int32 [8], replicated, may hold values from 4 to 8
- coupling: float32 [4, 8, 8], replicated, may hold values from -0.4 to 2, as said below
Outputs:
- forces: float32 [3, 8], P(None, 'band')
- stress: float32 [3, 3], replicated
Inputs may be any that keep to these rules, and one draw needn't show every extreme that they name: `coupling`: symmetric in its last two dimensions.
All inputs are finite; a program needn't handle non-finite values.
Results may differ from a plain program's by a relative error of at most 0.006.
Values may be sent and summed in bfloat16 or wider, within the bound.
A program may use at most 64 MiB of HBM per device.

v0:
```python
import math
import jax
import jax.numpy as jnp
from jax import lax
from jax.sharding import PartitionSpec as P

PROJ = 8
MILLER = 24
stress_pairs = ((0, 0), (1, 1), (2, 2), (0, 1), (0, 2), (1, 2))


def cart_weights(miller_index, lattice):
    indices = miller_index.astype(jnp.float32)
    coords = []
    for column in range(3):
        coords.append(
            (
                indices[0] * lattice[0, column]
                + indices[1] * lattice[1, column]
                + indices[2] * lattice[2, column]
            )
            / MILLER
        )
    isotropic = (coords[0] * coords[0] + coords[1] * coords[1] + coords[2] * coords[2]) / 3.0
    weight_rows = [jnp.ones_like(coords[0])] + coords
    for first_axis, second_axis in stress_pairs:
        product = coords[first_axis] * coords[second_axis]
        if first_axis == second_axis:
            product = product - isotropic
        weight_rows.append(product)
    return jnp.stack(weight_rows)


def scale_block(weights, atom_block):
    proj_rows = atom_block.shape[1]
    scaled = (weights[:, None, None, :] * atom_block[None].astype(jnp.float32)).astype(jnp.bfloat16)
    return scaled.reshape(20 * proj_rows, atom_block.shape[2])


def intersection(scaled, flat_waves):
    product = lax.dot_general(
        scaled, flat_waves, (((1,), (1,)), ((), ())), preferred_element_type=jnp.float32
    )
    product = product.reshape(10, 2, scaled.shape[0] // 20, 2, flat_waves.shape[0] // 2)
    real_part = product[:, 0, :, 0] + product[:, 1, :, 1]
    imag_part = product[:, 0, :, 1] - product[:, 1, :, 0]
    return jnp.stack([real_part, imag_part], axis=1)


def atom_couplings(species, proj_count, coupling):
    kind_count = coupling.shape[0]
    proj_width = coupling.shape[1]
    onehot = (species[:, None] == jnp.arange(kind_count, dtype=jnp.int32)[None, :]).astype(
        jnp.float32
    )
    chosen = jnp.einsum("as,sij->aij", onehot, coupling, precision=lax.Precision.HIGHEST)
    active = (jnp.arange(proj_width, dtype=jnp.int32)[None, :] < proj_count[:, None]).astype(
        jnp.float32
    )
    return chosen * active[:, :, None] * active[:, None, :]


def contract(per_atom, couplings, occupied):
    mixed = jnp.einsum("aij,kcajn->kcain", couplings, per_atom, precision=lax.Precision.HIGHEST)
    becp_real = per_atom[0, 0]
    becp_imag = per_atom[0, 1]
    imag_sum = jnp.sum(becp_real[None] * mixed[1:4, 1] - becp_imag[None] * mixed[1:4, 0], axis=2)
    real_sum = jnp.sum(becp_real[None] * mixed[4:, 0] + becp_imag[None] * mixed[4:, 1], axis=2)
    force_part = jnp.sum(imag_sum * occupied, axis=2)
    stress_part = jnp.sum(real_sum * occupied, axis=(1, 2))
    return (force_part, stress_part)


def stress_matrix(values):
    return jnp.stack(
        [
            jnp.stack([values[0], values[3], values[4]]),
            jnp.stack([values[3], values[1], values[5]]),
            jnp.stack([values[4], values[5], values[2]]),
        ]
    )


def body(wave_coeffs, projectors, miller_index, lattice, occupation, species, proj_count, coupling):
    weights = cart_weights(miller_index, lattice)
    band_count = wave_coeffs.shape[1]
    quarter_count = band_count // lax.axis_size("gvec")
    group_slot = lax.axis_index("gvec")
    atom_total = species.shape[0]
    flat_waves = wave_coeffs.reshape(2 * band_count, wave_coeffs.shape[2])
    total_proj = PROJ * lax.axis_size("band")
    start_carry = jnp.zeros((band_count, 10, 2, total_proj), jnp.float32)
    arrived = lax.all_gather(projectors, "band", axis=1, tiled=True)
    block_rows = arrived.shape[1]
    anchor = jnp.zeros((), jnp.int32)

    def one_atom(atom_slot, partial_value):
        atom_block = lax.dynamic_slice_in_dim(arrived, atom_slot * PROJ, PROJ, 1)
        values = intersection(scale_block(weights, atom_block), flat_waves).transpose(3, 0, 1, 2)
        return lax.dynamic_update_slice(
            partial_value, values, (anchor, anchor, anchor, atom_slot * PROJ)
        )

    intersections = lax.fori_loop(0, block_rows // PROJ, one_atom, start_carry)
    couplings = atom_couplings(species, proj_count, coupling)
    owned_rows = lax.psum_scatter(intersections, "gvec", scatter_dimension=0, tiled=True)
    occupied = lax.dynamic_slice_in_dim(occupation, group_slot * quarter_count, quarter_count, 0)
    per_atom = owned_rows.reshape(quarter_count, 10, 2, atom_total, PROJ).transpose(1, 2, 3, 4, 0)
    force_part, stress_part = contract(per_atom, couplings, occupied)
    band_total = band_count * lax.axis_size("band")
    force_scale = 2.0 / (PROJ * math.sqrt(band_total))
    stress_scale = 1.0 / (PROJ * math.sqrt(atom_total * band_total))
    all_force, total_stress = lax.psum((force_part, stress_part), ("band", "gvec"))
    owned_atoms = atom_total // lax.axis_size("band")
    own_force = lax.dynamic_slice_in_dim(
        all_force, lax.axis_index("band") * owned_atoms, owned_atoms, 1
    )
    return (own_force * force_scale, stress_matrix(total_stress * stress_scale))


def solution(mesh):
    return jax.shard_map(
        body,
        mesh=mesh,
        in_specs=(
            P(None, "band", "gvec"),
            P(None, "band", "gvec"),
            P(None, "gvec"),
            P(),
            P("band"),
            P(),
            P(),
            P(),
        ),
        out_specs=(P(None, "band"), P()),
        check_vma=False,
    )
```

profile of v0, /device:TPU:0, one launch (start us, length us, event | category | flops | bytes accessed | tf_op | source)
XLA Modules:
  0.0 217.9 jit_solution(4178742472580967056)
XLA Ops:
  8.0 1.7 fusion.27
  11.5 1.2 dynamic-slice
  14.1 4.2 %fusion.25 = (f32[1,18816]{1,0:T(1,128)S(1)}, f32[1,18816]{1,0:T(1,128)S(1)}, f32[1,18816]{1,0:T(1,128)S(1)}) fusion(f32[]{:T(128)} %bitcast.16, f32[3,18816]{1,0:T(4,128)S(1)} %convert_element_type.32, f32[]{:T(128)} %bitcast.15, f32[]{:T(128)} %bitcast.14, f32[]{:T(128)} %bitcast.13, f32[]{:T(128)} %bitcast.12, f32[]{:T(128)} %bitcast.11), kind=kLoop, calls=%fused_computation.55 | loop fusion | flops 244608 | bytes 451608 | tf_op jit(solution)/shard_map/mul | solution.py:27
  18.3 2.1 fusion.26
  20.8 1.3 stack.48
  22.0 71.5 %all-gather.2.cloned.1.call-done = bf16[2,64,18816]{2,1,0:T(8,128)(2,1)} async-done(((bf16[2,8,18816]{2,1,0:T(8,128)(2,1)}), bf16[2,64,18816]{2,1,0:T(8,128)(2,1)}) %all-gather.2.cloned.1.call-update) | async-done | bytes 4816912 | tf_op jit(solution)/shard_map/all_gather | solution.py:93
  93.6 37.3 %while.13 = (s32[]{:T(128)}, f32[32,10,2,64]{0,3,1,2:T(8,128)S(1)}, f32[10,18816]{1,0:T(8,128)S(1)}, bf16[2,64,18816]{2,1,0:T(8,128)(2,1)}, bf16[64,18816]{1,0:T...) while((s32[]{:T(128)}, f32[32,10,2,64]{0,3,1,2:T(8,128)S(1)}, f32[10,18816]{1,0:T(8,128)S(1)}, ...), condition=%wide.region_1.0_spmd, body=%wide.region_0.0_spmd.sunk | while | flops 391684096 | bytes 6438035 | solution.py:104
  93.6 1.2 dynamic-slice_convert_fusion.2
  94.8 3.4 %fusion.40 = f32[10,2,8,2,32]{4,2,3,1,0:T(8,128)S(1)} fusion(bf16[2,32,18816,1,1]{2,1,0,4,3:T(8,128)(2,1)} %bitcast.110, f32[2,8,18816]{2,1,0:T(8,128)S(1)} %dynamic-slice_convert_fusion.2, f32[10,18816]{1,0:T(8,128)S(1)} %get-tuple-element.190), kind=kOutput, calls=%fused_computation.2.clone.1 | convolution fusion | flops 391372800 | bytes 4406272 | tf_op jit(solution)/shard_map/while/body/eval_jaxpr/dot_general | solution.py:41
  98.3 1.2 dynamic-slice_convert_fusion.2
  99.4 3.4 %fusion.40 = f32[10,2,8,2,32]{4,2,3,1,0:T(8,128)S(1)} fusion(bf16[2,32,18816,1,1]{2,1,0,4,3:T(8,128)(2,1)} %bitcast.110, f32[2,8,18816]{2,1,0:T(8,128)S(1)} %dynamic-slice_convert_fusion.2, f32[10,18816]{1,0:T(8,128)S(1)} %get-tuple-element.190), kind=kOutput, calls=%fused_computation.2.clone.1 | convolution fusion | flops 391372800 | bytes 4406272 | tf_op jit(solution)/shard_map/while/body/eval_jaxpr/dot_general | solution.py:41
  102.9 1.2 dynamic-slice_convert_fusion.2
  104.1 3.4 %fusion.40 = f32[10,2,8,2,32]{4,2,3,1,0:T(8,128)S(1)} fusion(bf16[2,32,18816,1,1]{2,1,0,4,3:T(8,128)(2,1)} %bitcast.110, f32[2,8,18816]{2,1,0:T(8,128)S(1)} %dynamic-slice_convert_fusion.2, f32[10,18816]{1,0:T(8,128)S(1)} %get-tuple-element.190), kind=kOutput, calls=%fused_computation.2.clone.1 | convolution fusion | flops 391372800 | bytes 4406272 | tf_op jit(solution)/shard_map/while/body/eval_jaxpr/dot_general | solution.py:41
  107.6 1.2 dynamic-slice_convert_fusion.2
  108.7 3.4 %fusion.40 = f32[10,2,8,2,32]{4,2,3,1,0:T(8,128)S(1)} fusion(bf16[2,32,18816,1,1]{2,1,0,4,3:T(8,128)(2,1)} %bitcast.110, f32[2,8,18816]{2,1,0:T(8,128)S(1)} %dynamic-slice_convert_fusion.2, f32[10,18816]{1,0:T(8,128)S(1)} %get-tuple-element.190), kind=kOutput, calls=%fused_computation.2.clone.1 | convolution fusion | flops 391372800 | bytes 4406272 | tf_op jit(solution)/shard_map/while/body/eval_jaxpr/dot_general | solution.py:41
  112.2 1.2 dynamic-slice_convert_fusion.2
  113.4 3.4 %fusion.40 = f32[10,2,8,2,32]{4,2,3,1,0:T(8,128)S(1)} fusion(bf16[2,32,18816,1,1]{2,1,0,4,3:T(8,128)(2,1)} %bitcast.110, f32[2,8,18816]{2,1,0:T(8,128)S(1)} %dynamic-slice_convert_fusion.2, f32[10,18816]{1,0:T(8,128)S(1)} %get-tuple-element.190), kind=kOutput, calls=%fused_computation.2.clone.1 | convolution fusion | flops 391372800 | bytes 4406272 | tf_op jit(solution)/shard_map/while/body/eval_jaxpr/dot_general | solution.py:41
  118.1 3.4 %fusion.40 = f32[10,2,8,2,32]{4,2,3,1,0:T(8,128)S(1)} fusion(bf16[2,32,18816,1,1]{2,1,0,4,3:T(8,128)(2,1)} %bitcast.110, f32[2,8,18816]{2,1,0:T(8,128)S(1)} %dynamic-slice_convert_fusion.2, f32[10,18816]{1,0:T(8,128)S(1)} %get-tuple-element.190), kind=kOutput, calls=%fused_computation.2.clone.1 | convolution fusion | flops 391372800 | bytes 4406272 | tf_op jit(solution)/shard_map/while/body/eval_jaxpr/dot_general | solution.py:41
  122.7 3.4 %fusion.40 = f32[10,2,8,2,32]{4,2,3,1,0:T(8,128)S(1)} fusion(bf16[2,32,18816,1,1]{2,1,0,4,3:T(8,128)(2,1)} %bitcast.110, f32[2,8,18816]{2,1,0:T(8,128)S(1)} %dynamic-slice_convert_fusion.2, f32[10,18816]{1,0:T(8,128)S(1)} %get-tuple-element.190), kind=kOutput, calls=%fused_computation.2.clone.1 | convolution fusion | flops 391372800 | bytes 4406272 | tf_op jit(solution)/shard_map/while/body/eval_jaxpr/dot_general | solution.py:41
  126.2 1.2 dynamic-slice_convert_fusion.2
  127.4 3.4 %fusion.40 = f32[10,2,8,2,32]{4,2,3,1,0:T(8,128)S(1)} fusion(bf16[2,32,18816,1,1]{2,1,0,4,3:T(8,128)(2,1)} %bitcast.110, f32[2,8,18816]{2,1,0:T(8,128)S(1)} %dynamic-slice_convert_fusion.2, f32[10,18816]{1,0:T(8,128)S(1)} %get-tuple-element.190), kind=kOutput, calls=%fused_computation.2.clone.1 | convolution fusion | flops 391372800 | bytes 4406272 | tf_op jit(solution)/shard_map/while/body/eval_jaxpr/dot_general | solution.py:41
  132.1 30.9 %all-reduce.4.cloned.1.call-done = f32[32,10,2,64]{3,2,1,0:T(2,128)} async-done(((f32[32,10,2,64]{3,2,1,0:T(2,128)}), f32[32,10,2,64]{3,2,1,0:T(2,128)}) %all-reduce.4.cloned.1.call-update) | async-done | bytes 163856
  166.6 39.4 %all-reduce.1 = (f32[3,8]{0,1:T(8,128)S(1)}, f32[6]{0:T(128)S(1)}) all-reduce(f32[3,8]{0,1:T(8,128)S(1)} %multiply_reduce_fusion.1, f32[6]{0:T(128)S(1)} %multiply_reduce_fusion), channel_id=1, replica_groups=mesh['band'=8,'gvec'=4] {'band','gvec'}, use_global_device_ids=true, to_apply=%region_5.0 | all-reduce | flops 30 | bytes 240 | tf_op jit(solution)/shard_map/psum | solution.py:113
  207.9 2.6 %maximum_bitcast_fusion.1 = (f32[1,3]{1,0:T(1,128)S(1)}, f32[1,3]{1,0:T(1,128)S(1)}) fusion(f32[2]{0:T(128)S(1)} %get-tuple-element.135, f32[1]{0:T(128)} %get-tuple-element.130, f32[1]{0:T(128)} %get-tuple-element.132, f32[1]{0:T(128)} %get-tuple-element.133, f32[1]{0:T(128)} %get-tuple-element.134), kind=kLoop, calls=%fused_computation.49 | loop fusion | flops 9 | bytes 48 | tf_op jit(solution)/shard_map/stack | solution.py:75
  (61 shorter events, 13.6 us)
Async XLA Ops:
  7.2 124.7 %copy-start = (f32[4,8,8]{2,1,0:T(8,128)S(1)}, f32[4,8,8]{2,1,0:T(8,128)}, u32[]{:S(2)}) copy-start(f32[4,8,8]{2,1,0:T(8,128)} %param.17) | copy-start | bytes 3076
  7.2 86.3 %all-gather.2.cloned.1.call-start = ((), (), s32[]{:S(2)}) async-start(), calls=%async_computation | async-start | bytes 5419008 | tf_op jit(solution)/shard_map/all_gather | solution.py:93
  7.9 155.0 %all-reduce.4.cloned.1.call-start = ((), (), s32[]{:S(2)}) async-start(), calls=%async_computation.1 | async-start | bytes 655360
  93.6 38.3 %copy-start.1 = (s32[8]{0:T(128)S(1)}, s32[8]{0:T(128)}, u32[]{:S(2)}) copy-start(s32[8]{0:T(128)} %param.15) | copy-start | bytes 100
Sparse Core Ops, SparseCore 0:
  10.2 83.2 all-gather.1
  132.0 30.9 all-reduce.3
where the time goes:
time: 219 us; the launch traced here: 218 us
  waiting for transfers between devices  103 us (47%)
  blocking collectives  39.4 us (18%)
  matrix products  28.2 us (13%)
  other arithmetic  23.1 us (11%)
  between operations  14.8 us (7%)
  local copies, waits for them, and re-layouts  8.95 us (4%)
    all_gather x1, waiting for transfers between devices, body(): arrived = lax.all_gather(projectors, 'band', axis=1, tiled=True)  71.5 us
    psum x1, blocking collectives, body(): lax.psum((force_part, stress_part), ('band', 'gvec'))  39.4 us
    unnamed x3, waiting for transfers between devices  31.5 us
    dot_general x8, matrix products, intersection(): lax.dot_general(scaled, flat_waves, (((1,), (1,)), ((), ())), preferred_e...  27.4 us
    convert_element_type x8, other arithmetic, scale_block(): atom_block[None].astype(jnp.float32)  9.23 us
    mul x2, other arithmetic, cart_weights(): product = coords[first_axis] * coords[second_axis]  6.28 us
  transfers between devices with their start and end apart: 2, of which 2 were waited for; matrix products, arithmetic and copies ran while one was open for 6% of the time, Pallas kernels for 0%

commit v1 on v0

--- a/solution.py
+++ b/solution.py
@@ -82,6 +82,10 @@
 
 
 def body(wave_coeffs, projectors, miller_index, lattice, occupation, species, proj_count, coupling):
+
+    def list_strings(work_x, named_axis, a_name):
+        return jax.lax.psum(jax.lax.psum(work_x, named_axis), a_name)
+
     weights = cart_weights(miller_index, lattice)
     band_count = wave_coeffs.shape[1]
     quarter_count = band_count // lax.axis_size("gvec")
@@ -110,7 +114,7 @@
     band_total = band_count * lax.axis_size("band")
     force_scale = 2.0 / (PROJ * math.sqrt(band_total))
     stress_scale = 1.0 / (PROJ * math.sqrt(atom_total * band_total))
-    all_force, total_stress = lax.psum((force_part, stress_part), ("band", "gvec"))
+    all_force, total_stress = list_strings((force_part, stress_part), "gvec", "band")
     owned_atoms = atom_total // lax.axis_size("band")
     own_force = lax.dynamic_slice_in_dim(
         all_force, lax.axis_index("band") * owned_atoms, owned_atoms, 1

time: 219 us -> 207 us (0.945)
  blocking collectives: 39.4 us -> 27.6 us
    psum x1 -> x2, blocking collectives: 39.4 us -> 27.6 us  [list_strings(): return jax.lax.psum(jax.lax.psum(work_x, named_axis), a_name)]
  transfers between devices with their start and end apart: 2 -> 2, of which waited for: 2 -> 2; matrix products, arithmetic and copies ran while one was open for 6% -> 7% of each run, Pallas kernels for 0% -> 0%
where the time goes in v1:
time: 207 us; the launch traced here: 206 us
  waiting for transfers between devices  103 us (50%)
  matrix products  28.2 us (14%)
  blocking collectives  27.6 us (13%)
  other arithmetic  23.1 us (11%)
  between operations  14.8 us (7%)
  local copies, waits for them, and re-layouts  8.98 us (4%)
    all_gather x1, waiting for transfers between devices, body(): arrived = lax.all_gather(projectors, 'band', axis=1, tiled=True)  71.4 us
    unnamed x3, waiting for transfers between devices  31.6 us
    psum x2, blocking collectives, list_strings(): return jax.lax.psum(jax.lax.psum(work_x, named_axis), a_name)  27.6 us
    dot_general x8, matrix products, intersection(): lax.dot_general(scaled, flat_waves, (((1,), (1,)), ((), ())), preferred_e...  27.4 us
    convert_element_type x8, other arithmetic, scale_block(): atom_block[None].astype(jnp.float32)  9.23 us
    mul x2, other arithmetic, cart_weights(): product = coords[first_axis] * coords[second_axis]  6.28 us
  transfers between devices with their start and end apart: 2, of which 2 were waited for; matrix products, arithmetic and copies ran while one was open for 7% of the time, Pallas kernels for 0%

profile of v1, /device:TPU:0, one launch (start us, length us, event | category | flops | bytes accessed | tf_op | source)
XLA Modules:
  0.0 206.2 jit_solution(15706976014731857109)
XLA Ops:
  8.0 1.7 fusion.27
  11.5 1.3 dynamic-slice
  14.1 4.2 %fusion.25 = (f32[1,18816]{1,0:T(1,128)S(1)}, f32[1,18816]{1,0:T(1,128)S(1)}, f32[1,18816]{1,0:T(1,128)S(1)}) fusion(f32[]{:T(128)} %bitcast.16, f32[3,18816]{1,0:T(4,128)S(1)} %convert_element_type.32, f32[]{:T(128)} %bitcast.15, f32[]{:T(128)} %bitcast.14, f32[]{:T(128)} %bitcast.13, f32[]{:T(128)} %bitcast.12, f32[]{:T(128)} %bitcast.11), kind=kLoop, calls=%fused_computation.55 | loop fusion | flops 244608 | bytes 451608 | tf_op jit(solution)/shard_map/mul | solution.py:27
  18.3 2.1 %fusion.26 = (f32[1,18816]{1,0:T(1,128)S(1)}, f32[1,18816]{1,0:T(1,128)S(1)}) fusion(f32[1,18816]{1,0:T(1,128)S(1)} %get-tuple-element.112, f32[]{:T(128)} %bitcast.10, f32[3,18816]{1,0:T(4,128)S(1)} %convert_element_type.32, f32[]{:T(128)} %bitcast.9, f32[]{:T(128)} %bitcast.8), kind=kLoop, calls=%fused_computation.56 | loop fusion | flops 131712 | bytes 451596 | tf_op jit(solution)/shard_map/mul | solution.py:27
  20.8 1.3 stack.48
  22.1 71.4 %all-gather.2.cloned.1.call-done = bf16[2,64,18816]{2,1,0:T(8,128)(2,1)} async-done(((bf16[2,8,18816]{2,1,0:T(8,128)(2,1)}), bf16[2,64,18816]{2,1,0:T(8,128)(2,1)}) %all-gather.2.cloned.1.call-update) | async-done | bytes 4816912 | tf_op jit(solution)/shard_map/all_gather | solution.py:97
  93.6 37.3 %while.13 = (s32[]{:T(128)}, f32[32,10,2,64]{0,3,1,2:T(8,128)S(1)}, f32[10,18816]{1,0:T(8,128)S(1)}, bf16[2,64,18816]{2,1,0:T(8,128)(2,1)}, bf16[64,18816]{1,0:T...) while((s32[]{:T(128)}, f32[32,10,2,64]{0,3,1,2:T(8,128)S(1)}, f32[10,18816]{1,0:T(8,128)S(1)}, ...), condition=%wide.region_1.0_spmd, body=%wide.region_0.0_spmd.sunk | while | flops 391684096 | bytes 6438035 | solution.py:108
  93.6 1.2 dynamic-slice_convert_fusion.2
  94.8 3.4 %fusion.40 = f32[10,2,8,2,32]{4,2,3,1,0:T(8,128)S(1)} fusion(bf16[2,32,18816,1,1]{2,1,0,4,3:T(8,128)(2,1)} %bitcast.110, f32[2,8,18816]{2,1,0:T(8,128)S(1)} %dynamic-slice_convert_fusion.2, f32[10,18816]{1,0:T(8,128)S(1)} %get-tuple-element.192), kind=kOutput, calls=%fused_computation.2.clone.1 | convolution fusion | flops 391372800 | bytes 4406272 | tf_op jit(solution)/shard_map/while/body/eval_jaxpr/dot_general | solution.py:41
  98.3 1.2 dynamic-slice_convert_fusion.2
  99.4 3.4 %fusion.40 = f32[10,2,8,2,32]{4,2,3,1,0:T(8,128)S(1)} fusion(bf16[2,32,18816,1,1]{2,1,0,4,3:T(8,128)(2,1)} %bitcast.110, f32[2,8,18816]{2,1,0:T(8,128)S(1)} %dynamic-slice_convert_fusion.2, f32[10,18816]{1,0:T(8,128)S(1)} %get-tuple-element.192), kind=kOutput, calls=%fused_computation.2.clone.1 | convolution fusion | flops 391372800 | bytes 4406272 | tf_op jit(solution)/shard_map/while/body/eval_jaxpr/dot_general | solution.py:41
  102.9 1.2 dynamic-slice_convert_fusion.2
  104.1 3.4 %fusion.40 = f32[10,2,8,2,32]{4,2,3,1,0:T(8,128)S(1)} fusion(bf16[2,32,18816,1,1]{2,1,0,4,3:T(8,128)(2,1)} %bitcast.110, f32[2,8,18816]{2,1,0:T(8,128)S(1)} %dynamic-slice_convert_fusion.2, f32[10,18816]{1,0:T(8,128)S(1)} %get-tuple-element.192), kind=kOutput, calls=%fused_computation.2.clone.1 | convolution fusion | flops 391372800 | bytes 4406272 | tf_op jit(solution)/shard_map/while/body/eval_jaxpr/dot_general | solution.py:41
  107.6 1.2 dynamic-slice_convert_fusion.2
  108.7 3.4 %fusion.40 = f32[10,2,8,2,32]{4,2,3,1,0:T(8,128)S(1)} fusion(bf16[2,32,18816,1,1]{2,1,0,4,3:T(8,128)(2,1)} %bitcast.110, f32[2,8,18816]{2,1,0:T(8,128)S(1)} %dynamic-slice_convert_fusion.2, f32[10,18816]{1,0:T(8,128)S(1)} %get-tuple-element.192), kind=kOutput, calls=%fused_computation.2.clone.1 | convolution fusion | flops 391372800 | bytes 4406272 | tf_op jit(solution)/shard_map/while/body/eval_jaxpr/dot_general | solution.py:41
  112.2 1.2 dynamic-slice_convert_fusion.2
  113.4 3.4 %fusion.40 = f32[10,2,8,2,32]{4,2,3,1,0:T(8,128)S(1)} fusion(bf16[2,32,18816,1,1]{2,1,0,4,3:T(8,128)(2,1)} %bitcast.110, f32[2,8,18816]{2,1,0:T(8,128)S(1)} %dynamic-slice_convert_fusion.2, f32[10,18816]{1,0:T(8,128)S(1)} %get-tuple-element.192), kind=kOutput, calls=%fused_computation.2.clone.1 | convolution fusion | flops 391372800 | bytes 4406272 | tf_op jit(solution)/shard_map/while/body/eval_jaxpr/dot_general | solution.py:41
  118.1 3.4 %fusion.40 = f32[10,2,8,2,32]{4,2,3,1,0:T(8,128)S(1)} fusion(bf16[2,32,18816,1,1]{2,1,0,4,3:T(8,128)(2,1)} %bitcast.110, f32[2,8,18816]{2,1,0:T(8,128)S(1)} %dynamic-slice_convert_fusion.2, f32[10,18816]{1,0:T(8,128)S(1)} %get-tuple-element.192), kind=kOutput, calls=%fused_computation.2.clone.1 | convolution fusion | flops 391372800 | bytes 4406272 | tf_op jit(solution)/shard_map/while/body/eval_jaxpr/dot_general | solution.py:41
  122.7 3.4 %fusion.40 = f32[10,2,8,2,32]{4,2,3,1,0:T(8,128)S(1)} fusion(bf16[2,32,18816,1,1]{2,1,0,4,3:T(8,128)(2,1)} %bitcast.110, f32[2,8,18816]{2,1,0:T(8,128)S(1)} %dynamic-slice_convert_fusion.2, f32[10,18816]{1,0:T(8,128)S(1)} %get-tuple-element.192), kind=kOutput, calls=%fused_computation.2.clone.1 | convolution fusion | flops 391372800 | bytes 4406272 | tf_op jit(solution)/shard_map/while/body/eval_jaxpr/dot_general | solution.py:41
  127.4 3.4 %fusion.40 = f32[10,2,8,2,32]{4,2,3,1,0:T(8,128)S(1)} fusion(bf16[2,32,18816,1,1]{2,1,0,4,3:T(8,128)(2,1)} %bitcast.110, f32[2,8,18816]{2,1,0:T(8,128)S(1)} %dynamic-slice_convert_fusion.2, f32[10,18816]{1,0:T(8,128)S(1)} %get-tuple-element.192), kind=kOutput, calls=%fused_computation.2.clone.1 | convolution fusion | flops 391372800 | bytes 4406272 | tf_op jit(solution)/shard_map/while/body/eval_jaxpr/dot_general | solution.py:41
  132.1 30.9 %all-reduce.5.cloned.1.call-done = f32[32,10,2,64]{3,2,1,0:T(2,128)} async-done(((f32[32,10,2,64]{3,2,1,0:T(2,128)}), f32[32,10,2,64]{3,2,1,0:T(2,128)}) %all-reduce.5.cloned.1.call-update) | async-done | bytes 163856
  166.6 5.9 %all-reduce.2 = (f32[3,8]{0,1:T(8,128)S(1)}, f32[6]{0:T(128)S(1)}) all-reduce(f32[3,8]{0,1:T(8,128)S(1)} %multiply_reduce_fusion.1, f32[6]{0:T(128)S(1)} %multiply_reduce_fusion), channel_id=1, replica_groups=mesh['band'=8,'gvec'=4] {'gvec'}, use_global_device_ids=true, to_apply=%region_5.0 | all-reduce | flops 30 | bytes 240 | tf_op jit(solution)/shard_map/psum | solution.py:87
  172.4 21.8 %all-reduce.1 = (f32[3,8]{0,1:T(8,128)S(1)}, f32[6]{0:T(128)S(1)}) all-reduce(f32[3,8]{0,1:T(8,128)S(1)} %get-tuple-element.109, f32[6]{0:T(128)S(1)} %get-tuple-element.110), channel_id=1, replica_groups=mesh['band'=8,'gvec'=4] {'band'}, use_global_device_ids=true, to_apply=%region_6.0 | all-reduce | flops 30 | bytes 240 | tf_op jit(solution)/shard_map/psum | solution.py:87
  196.2 2.6 %maximum_bitcast_fusion.1 = (f32[1,3]{1,0:T(1,128)S(1)}, f32[1,3]{1,0:T(1,128)S(1)}) fusion(f32[2]{0:T(128)S(1)} %get-tuple-element.137, f32[1]{0:T(128)} %get-tuple-element.132, f32[1]{0:T(128)} %get-tuple-element.134, f32[1]{0:T(128)} %get-tuple-element.135, f32[1]{0:T(128)} %get-tuple-element.136), kind=kLoop, calls=%fused_computation.49 | loop fusion | flops 9 | bytes 48 | tf_op jit(solution)/shard_map/stack | solution.py:75
  (62 shorter events, 14.8 us)
Async XLA Ops:
  7.2 124.7 %copy-start = (f32[4,8,8]{2,1,0:T(8,128)S(1)}, f32[4,8,8]{2,1,0:T(8,128)}, u32[]{:S(2)}) copy-start(f32[4,8,8]{2,1,0:T(8,128)} %param.17) | copy-start | bytes 3076
  7.2 86.3 %all-gather.2.cloned.1.call-start = ((), (), s32[]{:S(2)}) async-start(), calls=%async_computation | async-start | bytes 5419008 | tf_op jit(solution)/shard_map/all_gather | solution.py:97
  7.9 155.0 %all-reduce.5.cloned.1.call-start = ((), (), s32[]{:S(2)}) async-start(), calls=%async_computation.1 | async-start | bytes 655360
  93.6 38.3 %copy-start.1 = (s32[8]{0:T(128)S(1)}, s32[8]{0:T(128)}, u32[]{:S(2)}) copy-start(s32[8]{0:T(128)} %param.15) | copy-start | bytes 100
Sparse Core Ops, SparseCore 0:
  10.2 83.2 all-gather.1
  132.0 30.9 all-reduce.4
